TPU v7x, 256 devices: a whole 4x4x8 slice. The times are simulated.
256 devices in a mesh: mom: 16 (over x, y_hi, core), col: 16 (over z, y_lo).
Axes of the slice: x: 4, y: 4 (y_hi: 2, y_lo: 2; y = y_hi * 2 + y_lo), z: 8, core: 2. Of those that a mesh axis runs over, the one named last changes fastest.
Arguments:
- vertex: bfloat16 [32768, 32768], P('mom', 'col'), may hold values from -1 to 1, as said below
- sources: bfloat16 [128, 32768], P('col', 'mom'), may hold values from -6 to 6
- green_fn: float32 [32768], P('mom'), may hold values from -1.2 to 1.2
- green_shifted: float32 [32768], P('mom'), may hold values from -1.2 to 1.2
- leg_weights: float32 [128], P('col'), may hold values from -0.25 to 0.25
Outputs:
- ladder: float32 [128, 32768], P('col', 'mom')
- dressed: float32 [32768], P('mom')
Inputs may be any that keep to these rules, and one draw needn't show every extreme that they name: vertex equals its own transpose.
All inputs are finite; a program needn't handle non-finite values.
Results may differ from a plain program's by a relative error of at most 0.0023.
Values may be sent and summed in bfloat16 or wider, within the bound.
A program may use at most 64 MiB of HBM per device.

v0:
```python
import jax
import jax.numpy as jnp
from jax import lax
from jax.sharding import PartitionSpec as P

SWEEPS = 3


def sent_to_all(shard, axis):
    peers = lax.axis_size(axis)
    return lax.all_to_all(
        jnp.broadcast_to(shard[None], (peers, *shard.shape)), axis, 0, 0, tiled=True
    )


def laid_out(blocks, dim):
    lengths = list(blocks.shape[1:])
    lengths[dim] *= blocks.shape[0]
    return jnp.moveaxis(blocks, 0, dim).reshape(lengths)


def gather_directly(shard, axis, dim):
    blocks = sent_to_all(shard, axis)
    return laid_out(blocks, dim)


def in_blocks(shard, dim, peers):
    lengths = shard.shape
    blocks = shard.reshape(*lengths[:dim], peers, lengths[dim] // peers, *lengths[dim + 1 :])
    return jnp.moveaxis(blocks, dim, 0)


def sum_at_owner(shard, axis, dim):
    blocks = in_blocks(shard, dim, lax.axis_size(axis))
    arrived = lax.all_to_all(blocks, axis, split_axis=0, concat_axis=0, tiled=True)
    return arrived.sum(axis=0)


def passed_along(block, axis, distance):
    devices = range(lax.axis_size(axis))
    route = [((i - distance) % len(devices), i) for i in devices]
    return lax.ppermute(block, axis, route)


def taken_together(shard, axis):
    everything = sent_to_all(shard, axis)
    return jnp.sum(everything, axis=0)


def body(vertex, sources, green_fn, green_shifted, leg_weights):
    mom_count = lax.axis_size("mom")
    col_count = lax.axis_size("col")
    shift_steps = mom_count // 4
    block_cols = vertex.shape[1]
    col_slice = sources.shape[0]
    total_cols = col_slice * col_count
    mom_slice = total_cols // mom_count
    mom_index = lax.axis_index("mom")
    col_index = lax.axis_index("col")
    source_here = sources.astype(jnp.float32)

    def relayout(narrow):
        gathered = gather_directly(narrow, "mom", 1)
        return lax.all_to_all(gathered, "col", split_axis=1, concat_axis=0, tiled=True)

    ahead_slab = passed_along(green_shifted, "mom", -shift_steps)
    dressed = green_fn
    ladder_state = source_here
    for round_index in range(2):
        behind_slab = passed_along(dressed, "mom", shift_steps)
        bubble_row = -0.5 * (dressed * ahead_slab + green_shifted * behind_slab)
        if round_index == 0:
            ladder_state = bubble_row[None, :] * source_here
        whole_bubble = gather_directly(bubble_row, "mom", 0)
        bubble_col = lax.dynamic_slice_in_dim(whole_bubble, col_index * block_cols, block_cols, 0)
        if round_index == 0:
            source_wide = relayout(sources)
            source_across = lax.dynamic_slice_in_dim(
                source_wide, mom_index * mom_slice, mom_slice, 0
            ).astype(jnp.float32)
            operand = (bubble_col[None, :] * source_wide.astype(jnp.float32)).astype(jnp.bfloat16)
        else:
            operand = relayout(ladder_state.astype(jnp.bfloat16))
        tall_rows = operand
        for sweep_index in range(SWEEPS):
            if sweep_index % 2 == 0:
                ladder_state = bubble_row[None, :] * (
                    source_here
                    + sum_at_owner(
                        lax.dot_general(
                            operand,
                            vertex,
                            (((1,), (1,)), ((), ())),
                            preferred_element_type=jnp.float32,
                        ),
                        "col",
                        0,
                    )
                )
                if sweep_index + 1 < SWEEPS:
                    tall_rows = gather_directly(ladder_state.astype(jnp.bfloat16), "col", 0)
            else:

                def across_term(first_row, row_count, tall_rows=tall_rows):
                    return jnp.dot(tall_rows, vertex, preferred_element_type=jnp.float32)

                summed = sum_at_owner(
                    across_term(jnp.int32(0), mom_slice * lax.axis_size("mom")), "mom", 0
                )
                across = bubble_col[None, :] * (source_across + summed)
                operand = gather_directly(across.astype(jnp.bfloat16), "mom", 0)
        if round_index == 0:
            self_part = jnp.dot(leg_weights, ladder_state, precision=lax.Precision.HIGHEST)
            self_energy = taken_together(self_part, "col")
            dressed = green_fn + green_fn * green_fn * self_energy
    return (ladder_state, dressed)


def solution(mesh):
    in_specs = (P("mom", "col"), P("col", "mom"), P("mom"), P("mom"), P("col"))
    out_specs = (P("col", "mom"), P("mom"))
    return jax.shard_map(body, mesh=mesh, in_specs=in_specs, out_specs=out_specs, check_vma=False)
```

profile of v0, /device:TPU:1, one launch (start us, length us, event | category | flops | bytes accessed | tf_op | source)
XLA Modules:
  0.0 394.2 jit_solution(14991855491622784143)
XLA Ops:
  0.6 0.0 copy-start
  0.6 2.1 collective-permute-start.1
  2.8 1.4 collective-permute-start
  4.1 1.2 collective-permute-done.1
  5.3 0.2 collective-permute-done
  5.5 0.7 add_multiply_fusion.1
  6.2 0.1 broadcast_in_dim.18
  6.3 16.4 %all_to_all.107 = f32[16,1,2048]{2,1,0:T(1,128)S(1)} all-to-all(f32[16,1,2048]{2,1,0:T(1,128)S(1)} %broadcast_in_dim.18), channel_id=1, replica_groups=mesh['mom'=16,'col'=16] {'mom'}, dimensions={0} | all-to-all | bytes 262144 | tf_op jit(solution)/shard_map/all_to_all | solution.py:11
  22.7 0.8 broadcast_in_dim.19
  23.5 14.8 %all_to_all.108 = bf16[16,8,2048]{2,1,0:T(8,128)(2,1)} all-to-all(bf16[16,8,2048]{2,1,0:T(8,128)(2,1)S(1)} %broadcast_in_dim.19), channel_id=1, replica_groups=mesh['mom'=16,'col'=16] {'mom'}, dimensions={0} | all-to-all | bytes 1048576 | tf_op jit(solution)/shard_map/all_to_all | solution.py:11
  38.3 8.4 %all-to-all-start.2 = ((bf16[8,16,2048]{2,0,1:T(8,128)(2,1)}), bf16[8,16,2048]{2,0,1:T(8,128)(2,1)S(1)}, u32[]{:S(2)}, u32[]{:S(2)}) async-start(bf16[8,16,2048]{2,0,1:T(8,128)(2,1)} %bitcast.1), calls=%async_computation.2 | async-start | bytes 1048576 | tf_op jit(solution)/shard_map/all_to_all | solution.py:64
  46.7 0.0 copy-start.1
  46.7 15.3 %all-to-all-done.2 = bf16[8,16,2048]{2,0,1:T(8,128)(2,1)S(1)} async-done(((bf16[8,16,2048]{2,0,1:T(8,128)(2,1)}), bf16[8,16,2048]{2,0,1:T(8,128)(2,1)S(1)}, u32[]{:S(2)}, u32[]{:S(2)}) %all-to-all-start.2) | async-done | bytes 524320 | tf_op jit(solution)/shard_map/all_to_all | solution.py:64
  62.0 6.3 %fusion.10 = f32[16,8,2048]{2,1,0:T(8,128)S(1)} fusion(bf16[2048,2048]{1,0:T(8,128)(2,1)} %param.5, bf16[8,16,2048]{2,0,1:T(8,128)(2,1)S(1)} %all-to-all-done.2, f32[2048]{0:T(1024)S(1)} %dynamic_slice.9), kind=kOutput, calls=%fused_computation.10 | convolution fusion | flops 1074528256 | bytes 9969664 | tf_op jit(solution)/shard_map/dot_general | solution.py:90
  68.3 30.9 %all_to_all.109 = f32[16,8,2048]{2,1,0:T(8,128)S(1)} all-to-all(f32[16,8,2048]{2,1,0:T(8,128)S(1)} %fusion.10), channel_id=1, replica_groups=mesh['mom'=16,'col'=16] {'col'}, dimensions={0} | all-to-all | bytes 2097152 | tf_op jit(solution)/shard_map/all_to_all | solution.py:35
  99.2 0.1 reduce_sum.63
  99.2 0.0 copy-done.1
  99.3 19.6 %all_to_all.110 = bf16[16,8,2048]{2,1,0:T(8,128)(2,1)S(1)} all-to-all(bf16[16,8,2048]{2,1,0:T(8,128)(2,1)S(1)} %broadcast_in_dim.20), channel_id=1, replica_groups=mesh['mom'=16,'col'=16] {'col'}, dimensions={0} | all-to-all | bytes 1048576 | tf_op jit(solution)/shard_map/all_to_all | solution.py:11
  118.9 5.6 %fusion.8 = f32[16,8,2048]{2,1,0:T(8,128)} fusion(bf16[16,8,2048]{2,1,0:T(8,128)(2,1)S(1)} %all_to_all.110, bf16[2048,2048]{1,0:T(8,128)(2,1)} %param.5), kind=kOutput, calls=%fused_computation.8 | convolution fusion | flops 1073741824 | bytes 9961472 | tf_op jit(solution)/shard_map/dot_general | solution.py:105
  124.5 8.4 %all-to-all-start.5 = ((f32[16,8,2048]{2,1,0:T(8,128)}), f32[16,8,2048]{2,1,0:T(8,128)S(1)}, u32[]{:S(2)}, u32[]{:S(2)}) async-start(f32[16,8,2048]{2,1,0:T(8,128)} %fusion.8), calls=%async_computation.5 | async-start | bytes 2097152 | tf_op jit(solution)/shard_map/all_to_all | solution.py:35
  132.9 16.9 %all-to-all-done.5 = f32[16,8,2048]{2,1,0:T(8,128)S(1)} async-done(((f32[16,8,2048]{2,1,0:T(8,128)}), f32[16,8,2048]{2,1,0:T(8,128)S(1)}, u32[]{:S(2)}, u32[]{:S(2)}) %all-to-all-start.5) | async-done | bytes 1048608 | tf_op jit(solution)/shard_map/all_to_all | solution.py:35
  149.9 0.1 reduce_sum.64
  150.0 15.1 %all_to_all.111 = bf16[16,8,2048]{2,1,0:T(8,128)(2,1)S(1)} all-to-all(bf16[16,8,2048]{2,1,0:T(8,128)(2,1)S(1)} %broadcast_in_dim.21), channel_id=1, replica_groups=mesh['mom'=16,'col'=16] {'mom'}, dimensions={0} | all-to-all | bytes 1048576 | tf_op jit(solution)/shard_map/all_to_all | solution.py:11
  165.1 6.3 %fusion.6 = f32[16,8,2048]{2,1,0:T(8,128)S(1)} fusion(bf16[16,8,2048]{2,1,0:T(8,128)(2,1)S(1)} %all_to_all.111, bf16[2048,2048]{1,0:T(8,128)(2,1)} %param.5), kind=kOutput, calls=%fused_computation.6 | convolution fusion | flops 1073741824 | bytes 9961472 | tf_op jit(solution)/shard_map/dot_general | solution.py:90
  171.4 29.6 %all_to_all.112 = f32[16,8,2048]{2,1,0:T(8,128)S(1)} all-to-all(f32[16,8,2048]{2,1,0:T(8,128)S(1)} %fusion.6), channel_id=1, replica_groups=mesh['mom'=16,'col'=16] {'col'}, dimensions={0} | all-to-all | bytes 2097152 | tf_op jit(solution)/shard_map/all_to_all | solution.py:35
  201.0 0.1 reduce_sum.65
  201.2 17.5 %all_to_all.113 = bf16[16,8,2048]{2,1,0:T(8,128)(2,1)} all-to-all(bf16[16,8,2048]{2,1,0:T(8,128)(2,1)S(1)} %broadcast_in_dim.24), channel_id=1, replica_groups=mesh['mom'=16,'col'=16] {'mom'}, dimensions={0} | all-to-all | bytes 1048576 | tf_op jit(solution)/shard_map/all_to_all | solution.py:11
  218.7 0.0 copy-start.2
  218.7 0.0 copy-start.3
  218.7 3.7 all-to-all-start.11
  222.4 0.0 copy-done
  222.4 0.2 fusion.26
  222.6 15.5 %all-to-all-done.11 = bf16[8,16,2048]{2,0,1:T(8,128)(2,1)S(1)} async-done(((bf16[8,16,2048]{2,0,1:T(8,128)(2,1)}), bf16[8,16,2048]{2,0,1:T(8,128)(2,1)S(1)}, u32[]{:S(2)}, u32[]{:S(2)}) %all-to-all-start.11) | async-done | bytes 524320 | tf_op jit(solution)/shard_map/all_to_all | solution.py:64
  238.1 0.7 broadcast_in_dim.22
  238.9 4.3 %all-to-all-start.8 = ((f32[16,1,2048]{2,1,0:T(1,128)}), f32[16,1,2048]{2,1,0:T(1,128)S(1)}, u32[]{:S(2)}, u32[]{:S(2)}) async-start(f32[16,1,2048]{2,1,0:T(1,128)} %broadcast_in_dim.22), calls=%async_computation.8 | async-start | bytes 262144 | tf_op jit(solution)/shard_map/all_to_all | solution.py:11
  243.1 7.2 %fusion.4 = f32[16,8,2048]{2,1,0:T(8,128)} fusion(bf16[2048,2048]{1,0:T(8,128)(2,1)} %param.5, bf16[8,16,2048]{2,0,1:T(8,128)(2,1)S(1)} %all-to-all-done.11), kind=kOutput, calls=%fused_computation.4 | convolution fusion | flops 1073741824 | bytes 9961472 | tf_op jit(solution)/shard_map/dot_general | solution.py:90
  250.4 1.2 all-to-all-done.8
  251.6 6.3 %all-to-all-start.12 = ((f32[16,8,2048]{2,1,0:T(8,128)}), f32[16,8,2048]{2,1,0:T(8,128)S(1)}, u32[]{:S(2)}, u32[]{:S(2)}) async-start(f32[16,8,2048]{2,1,0:T(8,128)} %fusion.4), calls=%async_computation.12 | async-start | bytes 2097152 | tf_op jit(solution)/shard_map/all_to_all | solution.py:35
  257.9 0.1 reduce_sum.66
  258.0 0.0 copy-done.2
  258.1 0.0 copy-start.4
  258.1 0.5 collective-permute-start.2
  258.5 3.3 collective-permute-done.2
  261.9 0.0 copy-done.3
  261.9 20.6 %all-to-all-done.12 = f32[16,8,2048]{2,1,0:T(8,128)S(1)} async-done(((f32[16,8,2048]{2,1,0:T(8,128)}), f32[16,8,2048]{2,1,0:T(8,128)S(1)}, u32[]{:S(2)}, u32[]{:S(2)}) %all-to-all-start.12) | async-done | bytes 1048608 | tf_op jit(solution)/shard_map/all_to_all | solution.py:35
  282.5 0.1 reduce_sum.67
  282.6 22.4 %all_to_all.114 = bf16[16,8,2048]{2,1,0:T(8,128)(2,1)S(1)} all-to-all(bf16[16,8,2048]{2,1,0:T(8,128)(2,1)S(1)} %broadcast_in_dim.25), channel_id=1, replica_groups=mesh['mom'=16,'col'=16] {'col'}, dimensions={0} | all-to-all | bytes 1048576 | tf_op jit(solution)/shard_map/all_to_all | solution.py:11
  305.0 0.7 broadcast_in_dim.23
  305.7 6.8 %all-to-all-start.9 = ((f32[16,1,2048]{2,1,0:T(1,128)}), f32[16,1,2048]{2,1,0:T(1,128)S(1)}, u32[]{:S(2)}, u32[]{:S(2)}) async-start(f32[16,1,2048]{2,1,0:T(1,128)} %broadcast_in_dim.23), calls=%async_computation.9 | async-start | bytes 262144 | tf_op jit(solution)/shard_map/all_to_all | solution.py:11
  312.5 5.6 %fusion.2 = f32[16,8,2048]{2,1,0:T(8,128)} fusion(bf16[16,8,2048]{2,1,0:T(8,128)(2,1)S(1)} %all_to_all.114, bf16[2048,2048]{1,0:T(8,128)(2,1)} %param.5), kind=kOutput, calls=%fused_computation.2 | convolution fusion | flops 1073741824 | bytes 9961472 | tf_op jit(solution)/shard_map/dot_general | solution.py:105
  318.1 2.0 all-to-all-done.9
  320.1 0.0 copy-done.4
  320.1 5.2 %all-to-all-start.14 = ((f32[16,8,2048]{2,1,0:T(8,128)}), f32[16,8,2048]{2,1,0:T(8,128)S(1)}, u32[]{:S(2)}, u32[]{:S(2)}) async-start(f32[16,8,2048]{2,1,0:T(8,128)} %fusion.2), calls=%async_computation.14 | async-start | bytes 2097152 | tf_op jit(solution)/shard_map/all_to_all | solution.py:35
  325.4 16.9 %all-to-all-done.14 = f32[16,8,2048]{2,1,0:T(8,128)S(1)} async-done(((f32[16,8,2048]{2,1,0:T(8,128)}), f32[16,8,2048]{2,1,0:T(8,128)S(1)}, u32[]{:S(2)}, u32[]{:S(2)}) %all-to-all-start.14) | async-done | bytes 1048608 | tf_op jit(solution)/shard_map/all_to_all | solution.py:35
  342.3 0.1 reduce_sum.68
  342.4 15.1 %all_to_all.115 = bf16[16,8,2048]{2,1,0:T(8,128)(2,1)S(1)} all-to-all(bf16[16,8,2048]{2,1,0:T(8,128)(2,1)S(1)} %broadcast_in_dim.26), channel_id=1, replica_groups=mesh['mom'=16,'col'=16] {'mom'}, dimensions={0} | all-to-all | bytes 1048576 | tf_op jit(solution)/shard_map/all_to_all | solution.py:11
  357.5 6.3 %fusion = f32[16,8,2048]{2,1,0:T(8,128)S(1)} fusion(bf16[16,8,2048]{2,1,0:T(8,128)(2,1)S(1)} %all_to_all.115, bf16[2048,2048]{1,0:T(8,128)(2,1)} %param.5), kind=kOutput, calls=%fused_computation | convolution fusion | flops 1073741824 | bytes 9961472 | tf_op jit(solution)/shard_map/dot_general | solution.py:90
  363.8 29.6 %all_to_all.116 = f32[16,8,2048]{2,1,0:T(8,128)S(1)} all-to-all(f32[16,8,2048]{2,1,0:T(8,128)S(1)} %fusion), channel_id=1, replica_groups=mesh['mom'=16,'col'=16] {'col'}, dimensions={0} | all-to-all | bytes 2097152 | tf_op jit(solution)/shard_map/all_to_all | solution.py:35
  393.5 0.1 reduce_sum.69
  393.5 0.6 fusion.24
  (14 shorter events, 0.3 us)
Async XLA Ops:
  0.6 221.8 %copy-start = (f32[8]{0:T(128)S(1)}, f32[8]{0:T(128)}, u32[]{:S(2)}) copy-start(f32[8]{0:T(128)} %param.9) | copy-start | bytes 100
  0.6 4.6 %collective-permute-start.1 = (f32[2048]{0:T(1024)}, f32[2048]{0:T(1024)S(1)}, u32[]{:S(2)}, u32[]{:S(2)}) collective-permute-start(f32[2048]{0:T(1024)} %param.7), channel_id=1, source_target_pairs={{192,0},{208,16},{224,32},{240,48},{0,64},{16,80},{32,96},{48,112}... | collective-permute-start | bytes 24584 | tf_op jit(solution)/shard_map/ppermute | solution.py:42
  2.8 2.7 collective-permute-start
  38.3 23.7 %all-to-all-start.2 = ((bf16[8,16,2048]{2,0,1:T(8,128)(2,1)}), bf16[8,16,2048]{2,0,1:T(8,128)(2,1)S(1)}, u32[]{:S(2)}, u32[]{:S(2)}) async-start(bf16[8,16,2048]{2,0,1:T(8,128)(2,1)} %bitcast.1), calls=%async_computation.2 | async-start | bytes 1048576 | tf_op jit(solution)/shard_map/all_to_all | solution.py:64
  46.7 52.6 %copy-start.1 = (bf16[8,2048]{1,0:T(8,128)(2,1)S(1)}, bf16[8,2048]{1,0:T(8,128)(2,1)}, u32[]{:S(2)}) copy-start(bf16[8,2048]{1,0:T(8,128)(2,1)} %param.6) | copy-start | bytes 98308
  124.5 25.3 %all-to-all-start.5 = ((f32[16,8,2048]{2,1,0:T(8,128)}), f32[16,8,2048]{2,1,0:T(8,128)S(1)}, u32[]{:S(2)}, u32[]{:S(2)}) async-start(f32[16,8,2048]{2,1,0:T(8,128)} %fusion.8), calls=%async_computation.5 | async-start | bytes 2097152 | tf_op jit(solution)/shard_map/all_to_all | solution.py:35
  218.7 39.4 %copy-start.2 = (f32[2048]{0:T(1024)S(1)}, f32[2048]{0:T(1024)}, u32[]{:S(2)}) copy-start(f32[2048]{0:T(1024)} %param.7) | copy-start | bytes 24580
  218.7 43.2 %copy-start.3 = (f32[2048]{0:T(1024)S(1)}, f32[2048]{0:T(1024)}, u32[]{:S(2)}) copy-start(f32[2048]{0:T(1024)} %param.8) | copy-start | bytes 24580
  218.7 19.5 %all-to-all-start.11 = ((bf16[8,16,2048]{2,0,1:T(8,128)(2,1)}), bf16[8,16,2048]{2,0,1:T(8,128)(2,1)S(1)}, u32[]{:S(2)}, u32[]{:S(2)}) async-start(bf16[8,16,2048]{2,0,1:T(8,128)(2,1)} %bitcast.8), calls=%async_computation.11 | async-start | bytes 1048576 | tf_op jit(solution)/shard_map/all_to_all | solution.py:64
  238.9 12.8 %all-to-all-start.8 = ((f32[16,1,2048]{2,1,0:T(1,128)}), f32[16,1,2048]{2,1,0:T(1,128)S(1)}, u32[]{:S(2)}, u32[]{:S(2)}) async-start(f32[16,1,2048]{2,1,0:T(1,128)} %broadcast_in_dim.22), calls=%async_computation.8 | async-start | bytes 262144 | tf_op jit(solution)/shard_map/all_to_all | solution.py:11
  251.6 30.8 %all-to-all-start.12 = ((f32[16,8,2048]{2,1,0:T(8,128)}), f32[16,8,2048]{2,1,0:T(8,128)S(1)}, u32[]{:S(2)}, u32[]{:S(2)}) async-start(f32[16,8,2048]{2,1,0:T(8,128)} %fusion.4), calls=%async_computation.12 | async-start | bytes 2097152 | tf_op jit(solution)/shard_map/all_to_all | solution.py:35
  258.1 62.1 %copy-start.4 = (f32[2048]{0:T(1024)}, f32[2048]{0:T(1024)S(1)}, u32[]{:S(2)}) copy-start(f32[2048]{0:T(1024)S(1)} %multiply_add_fusion) | copy-start | bytes 24580
  258.1 3.8 collective-permute-start.2
  305.7 14.4 %all-to-all-start.9 = ((f32[16,1,2048]{2,1,0:T(1,128)}), f32[16,1,2048]{2,1,0:T(1,128)S(1)}, u32[]{:S(2)}, u32[]{:S(2)}) async-start(f32[16,1,2048]{2,1,0:T(1,128)} %broadcast_in_dim.23), calls=%async_computation.9 | async-start | bytes 262144 | tf_op jit(solution)/shard_map/all_to_all | solution.py:11
  320.1 22.2 %all-to-all-start.14 = ((f32[16,8,2048]{2,1,0:T(8,128)}), f32[16,8,2048]{2,1,0:T(8,128)S(1)}, u32[]{:S(2)}, u32[]{:S(2)}) async-start(f32[16,8,2048]{2,1,0:T(8,128)} %fusion.2), calls=%async_computation.14 | async-start | bytes 2097152 | tf_op jit(solution)/shard_map/all_to_all | solution.py:35
where the time goes:
time: 396 us; the launch traced here: 394 us
  blocking collectives  211 us (53%)
  waiting for transfers between devices  93.2 us (24%)
  starting transfers between devices  47.1 us (12%)
  matrix products  37.5 us (9%)
    all_to_all x7, blocking collectives, sent_to_all(): lax.all_to_all(jnp.broadcast_to(shard[None], (peers, *shard.shape)), axis...  121 us
    all_to_all x3, blocking collectives, sum_at_owner(): lax.all_to_all(blocks, axis, split_axis=0, concat_axis=0, tiled=True)  90.2 us
    all_to_all x3, waiting for transfers between devices, sum_at_owner(): lax.all_to_all(blocks, axis, split_axis=0, concat_axis=0, tiled=True)  54.5 us
    all_to_all x2, waiting for transfers between devices, relayout(): lax.all_to_all(gathered, 'col', split_axis=1, concat_axis=0, tiled=True)  30.8 us
    dot_general x4, matrix products, body(): lax.dot_general(operand, vertex, (((1,), (1,)), ((), ())), preferred_elem...  26 us
    all_to_all x3, starting transfers between devices, sum_at_owner(): lax.all_to_all(blocks, axis, split_axis=0, concat_axis=0, tiled=True)  19.9 us
    all_to_all x2, starting transfers between devices, relayout(): lax.all_to_all(gathered, 'col', split_axis=1, concat_axis=0, tiled=True)  12.1 us
    dot_general x2, matrix products, across_term(): return jnp.dot(tall_rows, vertex, preferred_element_type=jnp.float32)  11.3 us
  transfers between devices with their start and end apart: 10, of which 10 were waited for; matrix products, arithmetic and copies ran while one was open for 3% of the time, Pallas kernels for 0%

commit v1 on v0

v1 whole, which is shorter than its diff:
```python
import functools

import jax
import jax.numpy as jnp
from jax import lax
from jax.experimental import pallas as pl
from jax.experimental.pallas import tpu as pltpu
from jax.sharding import PartitionSpec as P

MESH = pl.DeviceIdType.MESH
LANES = 128
ROWS = 8
F32 = jnp.float32
BF16 = jnp.bfloat16


class Axis:
    def __init__(self, name, which, size):
        self.name = name
        self.which = which
        self.size = size
        self.groups = size // 2
        self.me = lax.axis_index(name)
        self.parity = self.me % 2
        self.group = self.me // 2
        self.pair = self.me + 1 - 2 * self.parity

    def at(self, index):
        return {self.name: index}

    def mate(self, steps):
        return 2 * ((self.group + steps) % self.groups) + self.parity

    def order(self, k):
        sign = 2 * (k % 2) - 1
        return (self.groups // 2 + sign * ((k + 1) // 2) + self.groups) % self.groups


def remote(src, dst, send, recv, device):
    return pltpu.make_async_remote_copy(
        src_ref=src,
        dst_ref=dst,
        send_sem=send,
        recv_sem=recv,
        device_id=device,
        device_id_type=MESH,
    )


def loop(count, step):
    def run(k, carry):
        step(k)
        return carry

    lax.fori_loop(0, count, run, 0)


class Gather:
    def __init__(self, axis, buf, own, sems):
        self.axis, self.buf, self.own = axis, buf, own
        self.mate_send, self.mate_recv, self.pair_send, self.pair_recv = sems

    def mate_copy(self, t):
        a = self.axis
        return remote(
            self.own, self.buf.at[a.me], self.mate_send.at[t], self.mate_recv.at[t], a.at(a.mate(t))
        )

    def pair_copy(self, t, src):
        a = self.axis
        block = a.mate(a.groups - t)
        return remote(
            src, self.buf.at[block], self.pair_send.at[t], self.pair_recv.at[t], a.at(a.pair)
        )

    def start(self):
        a = self.axis
        self.pair_copy(0, self.own).start()
        loop(a.groups - 1, lambda k: self.mate_copy(a.order(k)).start())

    def forward(self, k):
        a = self.axis
        t = a.order(k)
        block = a.mate(a.groups - t)
        self.mate_copy(t).wait_recv()
        self.pair_copy(t, self.buf.at[block]).start()

    def forward_all(self):
        loop(self.axis.groups - 1, self.forward)

    def finish(self):
        a = self.axis

        def ended(k):
            t = a.order(k)
            copy = self.pair_copy(t, self.buf.at[a.me])
            copy.wait_recv()
            copy.wait_send()

        def sent(k):
            self.mate_copy(a.order(k)).wait_send()

        loop(a.groups, ended)
        loop(a.groups - 1, sent)


def kernel(
    size,
    ahead,
    v_hbm,
    src,
    g_in,
    s_in,
    w_in,
    lad_out,
    dre_out,
    v_mat,
    v_turned,
    x_mom,
    x_col,
    sbuf,
    wbuf,
    dvbuf,
    keep,
    give,
    taken,
    hand,
    landed,
    own,
    fin_wide,
    fin,
    fin_taken,
    fin_hand,
    fin_landed,
    b_full,
    s_ahead,
    g_behind,
    src_col,
    src_col_sent,
    src_mom,
    vec_sent,
    vec_mom,
    dre_sent,
    dre_behind,
    dv_sent,
    v_sem,
    shift_send,
    shift_recv,
    turn_send,
    turn_recv,
    behind_send,
    behind_recv,
    ag_sems,
    w_sems,
    dv_sems,
    rp_send,
    rp_recv,
    rg_send,
    rg_recv,
):
    mom = Axis("mom", 0, size)
    col = Axis("col", 1, size)
    groups = size // 2
    sources = size * ROWS
    block = size * LANES
    panel = 2 * LANES

    def v_copy(k):
        rows = pl.ds(pl.multiple_of(k * panel, panel), panel)
        return pltpu.make_async_copy(v_hbm.at[rows], v_mat.at[rows], v_sem.at[k])

    loop(groups, lambda k: v_copy(k).start())

    barrier = pltpu.get_barrier_semaphore()
    for a in (mom, col):
        pl.semaphore_signal(barrier, inc=1, device_id=a.at(a.pair), device_id_type=MESH)

        def greet(k, a=a):
            pl.semaphore_signal(barrier, inc=1, device_id=a.at(a.mate(k + 1)), device_id_type=MESH)

        loop(groups - 1, greet)
    turned = {"mom": col.me, "col": mom.me}
    off_diagonal = mom.me != col.me

    @pl.when(off_diagonal)
    def _():
        pl.semaphore_signal(barrier, inc=1, device_id=turned, device_id_type=MESH)

    @pl.when(off_diagonal)
    def _():
        pl.semaphore_wait(barrier, size + 1)

    @pl.when(jnp.logical_not(off_diagonal))
    def _():
        pl.semaphore_wait(barrier, size)

    def sems_of(ref, which):
        return tuple(ref.at[which, n] for n in range(4))

    to_behind = remote(
        s_in, s_ahead, shift_send.at[0], shift_recv.at[0], mom.at((mom.me + size - ahead) % size)
    )
    to_ahead = remote(g_in, g_behind, shift_send.at[1], shift_recv.at[1], mom.at((mom.me + ahead) % size))
    to_behind.start()
    to_ahead.start()
    source_gather = Gather(col, sbuf, src, sems_of(ag_sems, 1))
    source_gather.start()
    weight_gather = Gather(col, wbuf, w_in, sems_of(w_sems, 0))
    weight_gather.start()
    sbuf[col.me] = src[...]
    wbuf[col.me] = w_in[...]

    def turn_panel(k):
        v_copy(k).wait()
        rows = pl.ds(pl.multiple_of(k * panel, panel), panel)
        for n in range(groups):
            cols = slice(n * panel, (n + 1) * panel)
            v_turned[cols, rows] = v_mat[rows, cols].T

    def forward_and_turn(k):
        source_gather.forward(k)
        turn_panel(k)

    loop(groups - 1, forward_and_turn)
    turn_panel(groups - 1)
    weight_gather.forward_all()

    to_behind.wait()
    to_ahead.wait()
    b_full[...] = -0.5 * (g_in[...] * s_ahead[...] + s_in[...] * g_behind[...])
    source_gather.finish()

    def first_operand(k):
        two = sbuf[pl.ds(2 * k, 2)].astype(F32)
        rows = pl.ds(pl.multiple_of(2 * ROWS * k, 2 * ROWS), 2 * ROWS)
        for n in range(size):
            part = two[:, :, n * LANES : (n + 1) * LANES].reshape(2 * ROWS, LANES)
            x_col[n, rows, :] = (part * b_full[n : n + 1, :]).astype(BF16)

    loop(groups, first_operand)

    here = pl.ds(pl.multiple_of(col.me * LANES, LANES), LANES)
    mine = sbuf[:, :, here].astype(F32).reshape(sources, LANES)
    src_col[...] = mine
    src_col_sent[...] = mine.astype(BF16)
    for n, ref in enumerate((b_full, g_in, s_in, s_ahead)):
        vec_sent[n : n + 1, :] = ref[pl.ds(col.me, 1), :]
    vec_sent[4:8, :] = jnp.zeros((4, LANES), F32)
    src_turn = remote(src_col_sent, src_mom, turn_send.at[0], turn_recv.at[0], turned)
    vec_turn = remote(vec_sent, vec_mom, turn_send.at[1], turn_recv.at[1], turned)
    dv_turn = remote(dv_sent, dvbuf.at[mom.me], turn_send.at[2], turn_recv.at[2], turned)

    @pl.when(off_diagonal)
    def _():
        src_turn.start()
        vec_turn.start()

    def product(x, w, d):
        lhs = jnp.concatenate([x[n] for n in range(size)], axis=1)
        cols = pl.ds(pl.multiple_of(d * panel, panel), panel)
        return jnp.dot(lhs, w[:, cols], preferred_element_type=F32)

    def summed(a, x, w):
        def pair_copy(k):
            return remote(
                give.at[k], taken.at[a.which, k], rp_send.at[k], rp_recv.at[a.which, k], a.at(a.pair)
            )

        def mate_copy(k):
            t = a.order(k)
            return remote(
                hand.at[k],
                landed.at[a.which, t],
                rg_send.at[k],
                rg_recv.at[a.which, t],
                a.at(a.mate(t)),
            )

        first = a.parity == 0

        def multiply(k):
            both = product(x, w, (a.group + a.order(k)) % groups)
            low, high = both[:, :LANES], both[:, LANES:]
            keep[k] = jnp.where(first, low, high)
            give[k] = jnp.where(first, high, low).astype(BF16)
            pair_copy(k).start()

        loop(groups, multiply)

        def hand_on(k):
            pair_copy(k).wait_recv()
            hand[k] = (keep[k] + taken[a.which, k].astype(F32)).astype(BF16)
            mate_copy(k).start()

        loop(groups - 1, hand_on)
        pair_copy(groups - 1).wait_recv()
        total = keep[groups - 1] + taken[a.which, groups - 1].astype(F32)

        def add(k, total):
            mate_copy(k).wait_recv()
            return total + landed[a.which, a.order(k)].astype(F32)

        total = lax.fori_loop(0, groups - 1, add, total)

        def sent():
            loop(groups, lambda k: pair_copy(k).wait_send())
            loop(groups - 1, lambda k: mate_copy(k).wait_send())

        return total, sent

    mom_gather = Gather(mom, x_mom, x_mom.at[mom.me], sems_of(ag_sems, 0))
    col_gather = Gather(col, x_col, x_col.at[col.me], sems_of(ag_sems, 1))
    dv_gather = Gather(col, dvbuf, dvbuf.at[col.me], sems_of(dv_sems, 0))

    total, sent = summed(mom, x_col, v_mat)

    @pl.when(off_diagonal)
    def _():
        src_turn.wait()
        vec_turn.wait()

    @pl.when(jnp.logical_not(off_diagonal))
    def _():
        src_mom[...] = src_col_sent[...]
        vec_mom[...] = vec_sent[...]

    def mom_state(bubble, total):
        state = bubble * (src_mom[...].astype(F32) + total)
        x_mom[mom.me] = state.astype(BF16)
        return state

    def col_state(bubble, total):
        x_col[col.me] = (bubble * (src_col[...] + total)).astype(BF16)

    mom_state(vec_mom[0:1, :], total)
    mom_gather.start()
    sent()
    mom_gather.forward_all()
    mom_gather.finish()

    total, sent = summed(col, x_mom, v_turned)
    col_state(vec_sent[0:1, :], total)
    col_gather.start()
    sent()
    col_gather.forward_all()
    col_gather.finish()
    weight_gather.finish()

    total, sent = summed(mom, x_col, v_mat)
    ladder_first = mom_state(vec_mom[0:1, :], total)
    mom_gather.start()
    weights = wbuf[...].reshape(sources, LANES)
    self_energy = jnp.sum(weights * ladder_first, axis=0, keepdims=True)
    green = vec_mom[1:2, :]
    dressed = green + green * green * self_energy
    dre_sent[...] = jnp.broadcast_to(dressed, (ROWS, LANES))
    to_next = remote(dre_sent, dre_behind, behind_send, behind_recv, col.at((col.me + ahead) % size))
    to_next.start()
    sent()
    mom_gather.forward_all()
    to_next.wait()
    bubble_mom = -0.5 * (dressed * vec_mom[3:4, :] + vec_mom[2:3, :] * dre_behind[0:1, :])
    dv_sent[0:1, :] = dressed
    dv_sent[1:2, :] = bubble_mom
    dv_sent[2:8, :] = jnp.zeros((6, LANES), F32)

    @pl.when(off_diagonal)
    def _():
        dv_turn.start()

    mom_gather.finish()

    total, sent = summed(col, x_mom, v_turned)

    @pl.when(off_diagonal)
    def _():
        dv_turn.wait()

    @pl.when(jnp.logical_not(off_diagonal))
    def _():
        dvbuf[col.me] = dv_sent[...]

    col_state(dvbuf[col.me, 1:2, :], total)
    col_gather.start()
    dv_gather.start()
    sent()
    col_gather.forward_all()
    dv_gather.forward_all()
    col_gather.finish()

    total, sent = summed(mom, x_col, v_mat)
    mom_state(dv_sent[1:2, :], total)
    mom_gather.start()
    sent()
    mom_gather.forward_all()
    dv_gather.finish()
    mom_gather.finish()

    def last_product(d):
        both = product(x_mom, v_turned, d)
        cols = pl.ds(pl.multiple_of(d * panel, panel), panel)
        wide = both.reshape(size, ROWS, panel)
        fin_wide[:, :, cols] = wide
        fin[:, :, cols] = wide.astype(BF16)

    loop(groups, last_product)

    def fin_pair(k):
        there = col.mate(col.order(k)) + 1 - 2 * col.parity
        return remote(
            fin.at[there], fin_taken.at[k], rp_send.at[k], rp_recv.at[2, k], col.at(col.pair)
        )

    def fin_mate(k):
        t = col.order(k)
        return remote(
            fin_hand.at[k], fin_landed.at[t], rg_send.at[k], rg_recv.at[2, t], col.at(col.mate(t))
        )

    loop(groups, lambda k: fin_pair(k).start())

    def fin_sum(k):
        fin_pair(k).wait_recv()
        return fin_wide[col.mate(col.order(k))] + fin_taken[k].astype(F32)

    def fin_on(k):
        fin_hand[k] = fin_sum(k).astype(BF16)
        fin_mate(k).start()

    loop(groups - 1, fin_on)
    own[...] = fin_sum(groups - 1) + src[...].astype(F32)

    for n in range(size):
        dre_out[n : n + 1, :] = dvbuf[n, 0:1, :]

    def fin_add(k):
        fin_mate(k).wait_recv()
        own[...] += fin_landed[col.order(k)].astype(F32)

    loop(groups - 1, fin_add)
    for n in range(size):
        cols = slice(n * LANES, (n + 1) * LANES)
        lad_out[:, cols] = dvbuf[n, 1:2, :] * own[:, cols]

    loop(groups, lambda k: fin_pair(k).wait_send())
    loop(groups - 1, lambda k: fin_mate(k).wait_send())


def ladder_call(size, ahead):
    groups = size // 2
    sources = size * ROWS
    block = size * LANES
    slab = (sources, LANES)
    vmem = pl.BlockSpec(memory_space=pltpu.VMEM)
    dma = pltpu.SemaphoreType.DMA
    scratch = [
        pltpu.VMEM((block, block), BF16),
        pltpu.VMEM((block, block), BF16),
        pltpu.VMEM((size, *slab), BF16),
        pltpu.VMEM((size, *slab), BF16),
        pltpu.VMEM((size, ROWS, block), BF16),
        pltpu.VMEM((size, ROWS, LANES), F32),
        pltpu.VMEM((size, ROWS, LANES), F32),
        pltpu.VMEM((groups, *slab), F32),
        pltpu.VMEM((groups, *slab), BF16),
        pltpu.VMEM((2, groups, *slab), BF16),
        pltpu.VMEM((groups, *slab), BF16),
        pltpu.VMEM((2, groups, *slab), BF16),
        pltpu.VMEM((ROWS, block), F32),
        pltpu.VMEM((size, ROWS, block), F32),
        pltpu.VMEM((size, ROWS, block), BF16),
        pltpu.VMEM((groups, ROWS, block), BF16),
        pltpu.VMEM((groups, ROWS, block), BF16),
        pltpu.VMEM((groups, ROWS, block), BF16),
        pltpu.VMEM((size, LANES), F32),
        pltpu.VMEM((size, LANES), F32),
        pltpu.VMEM((size, LANES), F32),
        pltpu.VMEM(slab, F32),
        pltpu.VMEM(slab, BF16),
        pltpu.VMEM(slab, BF16),
        pltpu.VMEM((ROWS, LANES), F32),
        pltpu.VMEM((ROWS, LANES), F32),
        pltpu.VMEM((ROWS, LANES), F32),
        pltpu.VMEM((ROWS, LANES), F32),
        pltpu.VMEM((ROWS, LANES), F32),
        dma((groups,)),
        dma((2,)),
        dma((2,)),
        dma((3,)),
        dma((3,)),
        dma,
        dma,
        dma((2, 4, groups)),
        dma((1, 4, groups)),
        dma((1, 4, groups)),
        dma((groups,)),
        dma((3, groups)),
        dma((groups,)),
        dma((3, groups)),
    ]
    return pl.pallas_call(
        functools.partial(kernel, size, ahead),
        out_shape=(
            jax.ShapeDtypeStruct((ROWS, block), F32),
            jax.ShapeDtypeStruct((size, LANES), F32),
        ),
        in_specs=[pl.BlockSpec(memory_space=pl.ANY)] + [vmem] * 4,
        out_specs=(vmem, vmem),
        scratch_shapes=scratch,
        compiler_params=pltpu.CompilerParams(
            collective_id=0, has_side_effects=True, vmem_limit_bytes=48 * 1024 * 1024
        ),
        name="ladder",
    )


def body(ahead, vertex, sources, green_fn, green_shifted, leg_weights):
    size = lax.axis_size("mom")
    in_lanes = (size, LANES)
    ladder, dressed = ladder_call(size, ahead)(
        vertex,
        sources,
        green_fn.reshape(in_lanes),
        green_shifted.reshape(in_lanes),
        jnp.broadcast_to(leg_weights[:, None], (ROWS, LANES)),
    )
    return ladder, dressed.reshape(-1)


def solution(mesh):
    in_specs = (P("mom", "col"), P("col", "mom"), P("mom"), P("mom"), P("col"))
    out_specs = (P("col", "mom"), P("mom"))
    step = functools.partial(body, mesh.shape["mom"] // 4)
    return jax.shard_map(step, mesh=mesh, in_specs=in_specs, out_specs=out_specs, check_vma=False)
```

time: 396 us -> 142 us (0.36)
  blocking collectives: 211 us -> 0 us
  Pallas kernels: 0 us -> 137 us
  waiting for transfers between devices: 93.2 us -> 0 us
  starting transfers between devices: 47.1 us -> 0 us
  matrix products: 37.5 us -> 0 us
    all_to_all x10 -> x0, blocking collectives: 211 us -> none  [the longest x7 121 us: sent_to_all(): lax.all_to_all(jnp.broadcast_to(shard[None], (peers, *shard.shape)), axis...]
    pallas_call x0 -> x1, Pallas kernels: none -> 137 us  [body(): ladder_call(size, ahead)]
    all_to_all x7 -> x0, waiting for transfers between devices: 88.5 us -> none  [the longest x3 54.5 us: sum_at_owner(): lax.all_to_all(blocks, axis, split_axis=0, concat_axis=0, tiled=True)]
    all_to_all x7 -> x0, starting transfers between devices: 43.1 us -> none  [the longest x3 19.9 us: sum_at_owner(): lax.all_to_all(blocks, axis, split_axis=0, concat_axis=0, tiled=True)]
    dot_general x7 -> x0, matrix products: 37.5 us -> none  [the longest x4 26 us: body(): lax.dot_general(operand, vertex, (((1,), (1,)), ((), ())), preferred_elem...]
    ppermute x3 -> x0, waiting for transfers between devices: 4.67 us -> none  [passed_along(): return lax.ppermute(block, axis, route)]
  transfers between devices with their start and end apart: 10 -> 0, of which waited for: 10 -> 0; matrix products, arithmetic and copies ran while one was open for 3% -> 0% of each run, Pallas kernels for 0% -> 0%
where the time goes in v1:
time: 142 us
  Pallas kernels  137 us (96%)
  local copies, waits for them, and re-layouts  4.11 us (3%)
    pallas_call x1, Pallas kernels, body(): ladder_call(size, ahead)  137 us
    unnamed x8, local copies, waits for them, and re-layouts  3.38 us

profile of v1, /device:TPU:1, one launch (start us, length us, event | category | flops | bytes accessed | tf_op | source)
XLA Modules:
  0.0 142.1 jit_solution(17961955087488084640)
XLA Ops:
  0.6 0.7 broadcast_in_dim.2.w_in
  1.4 0.0 copy-start
  1.4 0.8 copy-done
  2.1 0.0 copy-start.1
  2.1 0.7 copy-done.1
  2.8 0.0 copy-start.2
  2.8 0.7 copy-done.2
  3.5 137.4 %ladder.1 = (f32[8,2048]{1,0:T(8,128)S(1)}, f32[16,128]{1,0:T(8,128)S(1)}) custom-call(bf16[2048,2048]{1,0:T(8,128)(2,1)} %v_hbm.1, bf16[8,2048]{1,0:T(8,128)(2,1)S(1)} %copy-done, f32[16,128]{1,0:T(8,128)S(1)} %bitcast.4, f32[16,128]{1,0:T(8,128)S(1)} %bitcast.5, f32[8,128]{1,0:T(8,128)S(1)} %broadcast_in_dim.2.w_in), custom_call_target="tpu_custom_call" | custom-call | tf_op jit(solution)/shard_map/ladder/pallas_call | solution.py:520
  140.9 0.6 copy.9
  141.5 0.6 copy.10
Async XLA Ops:
  1.4 0.8 copy-start
  2.1 0.7 copy-start.1
  2.8 0.7 copy-start.2

commit v2 on v1

--- a/solution.py
+++ b/solution.py
@@ -56,62 +56,60 @@
 
 
 class Gather:
-    def __init__(self, axis, buf, own, sems):
-        self.axis, self.buf, self.own = axis, buf, own
+    def __init__(self, axis, buf, sems, near):
+        self.axis, self.buf, self.near = axis, buf, near
         self.mate_send, self.mate_recv, self.pair_send, self.pair_recv = sems
+
+    def order(self, k):
+        a = self.axis
+        return a.order(a.groups - 2 - k) if self.near else a.order(k)
 
     def mate_copy(self, t):
         a = self.axis
-        return remote(
-            self.own, self.buf.at[a.me], self.mate_send.at[t], self.mate_recv.at[t], a.at(a.mate(t))
-        )
-
-    def pair_copy(self, t, src):
+        own = self.buf.at[a.me]
+        return remote(own, own, self.mate_send.at[t], self.mate_recv.at[t], a.at(a.mate(t)))
+
+    def pair_copy(self, t):
         a = self.axis
-        block = a.mate(a.groups - t)
-        return remote(
-            src, self.buf.at[block], self.pair_send.at[t], self.pair_recv.at[t], a.at(a.pair)
-        )
+        block = self.buf.at[a.mate(a.groups - t)]
+        return remote(block, block, self.pair_send.at[t], self.pair_recv.at[t], a.at(a.pair))
 
     def start(self):
-        a = self.axis
-        self.pair_copy(0, self.own).start()
-        loop(a.groups - 1, lambda k: self.mate_copy(a.order(k)).start())
+        self.pair_copy(0).start()
+        loop(self.axis.groups - 1, lambda k: self.mate_copy(self.order(k)).start())
 
     def forward(self, k):
-        a = self.axis
-        t = a.order(k)
-        block = a.mate(a.groups - t)
+        t = self.order(k)
         self.mate_copy(t).wait_recv()
-        self.pair_copy(t, self.buf.at[block]).start()
+        self.pair_copy(t).start()
 
     def forward_all(self):
         loop(self.axis.groups - 1, self.forward)
 
-    def finish(self):
+    def finish(self, use=None):
         a = self.axis
 
-        def ended(k):
-            t = a.order(k)
-            copy = self.pair_copy(t, self.buf.at[a.me])
-            copy.wait_recv()
-            copy.wait_send()
-
-        def sent(k):
-            self.mate_copy(a.order(k)).wait_send()
-
-        loop(a.groups, ended)
-        loop(a.groups - 1, sent)
+        def ended(t):
+            self.pair_copy(t).wait_recv()
+            if use is not None:
+                use((a.group - t + a.groups) % a.groups)
+
+        ended(0)
+        loop(a.groups - 1, lambda k: ended(self.order(k)))
+
+    def drain(self):
+        loop(self.axis.groups, lambda k: self.pair_copy(k).wait_send())
+        loop(self.axis.groups - 1, lambda k: self.mate_copy(k + 1).wait_send())
 
 
 def kernel(
     size,
     ahead,
     v_hbm,
-    src,
-    g_in,
-    s_in,
-    w_in,
+    src_hbm,
+    g_hbm,
+    s_hbm,
+    w_hbm,
     lad_out,
     dre_out,
     v_mat,
@@ -143,6 +141,10 @@
     dre_sent,
     dre_behind,
     dv_sent,
+    g_in,
+    s_in,
+    w_in,
+    in_sem,
     v_sem,
     shift_send,
     shift_recv,
@@ -169,30 +171,35 @@
         rows = pl.ds(pl.multiple_of(k * panel, panel), panel)
         return pltpu.make_async_copy(v_hbm.at[rows], v_mat.at[rows], v_sem.at[k])
 
-    loop(groups, lambda k: v_copy(k).start())
+    inputs = (
+        pltpu.make_async_copy(src_hbm, sbuf.at[col.me], in_sem.at[0]),
+        pltpu.make_async_copy(s_hbm, s_in, in_sem.at[1]),
+        pltpu.make_async_copy(g_hbm, g_in, in_sem.at[2]),
+        pltpu.make_async_copy(w_hbm, w_in, in_sem.at[3]),
+    )
+    for copy in inputs:
+        copy.start()
 
     barrier = pltpu.get_barrier_semaphore()
     for a in (mom, col):
-        pl.semaphore_signal(barrier, inc=1, device_id=a.at(a.pair), device_id_type=MESH)
 
         def greet(k, a=a):
-            pl.semaphore_signal(barrier, inc=1, device_id=a.at(a.mate(k + 1)), device_id_type=MESH)
-
-        loop(groups - 1, greet)
+            other = (a.me + k + 1) % size
+            pl.semaphore_signal(barrier, inc=1, device_id=a.at(other), device_id_type=MESH)
+
+        loop(size - 1, greet)
     turned = {"mom": col.me, "col": mom.me}
     off_diagonal = mom.me != col.me
 
-    @pl.when(off_diagonal)
-    def _():
-        pl.semaphore_signal(barrier, inc=1, device_id=turned, device_id_type=MESH)
-
-    @pl.when(off_diagonal)
-    def _():
-        pl.semaphore_wait(barrier, size + 1)
-
-    @pl.when(jnp.logical_not(off_diagonal))
-    def _():
-        pl.semaphore_wait(barrier, size)
+    loop(groups, lambda k: v_copy(k).start())
+    for copy in inputs:
+        copy.wait()
+    row = lax.broadcasted_iota(jnp.int32, (ROWS, LANES), 0)
+    weight_rows = jnp.zeros((ROWS, LANES), F32)
+    for n in range(ROWS):
+        weight_rows = jnp.where(row == n, w_in[n], weight_rows)
+    wbuf[col.me] = weight_rows
+    pl.semaphore_wait(barrier, 2 * (size - 1))
 
     def sems_of(ref, which):
         return tuple(ref.at[which, n] for n in range(4))
@@ -201,34 +208,28 @@
         s_in, s_ahead, shift_send.at[0], shift_recv.at[0], mom.at((mom.me + size - ahead) % size)
     )
     to_ahead = remote(g_in, g_behind, shift_send.at[1], shift_recv.at[1], mom.at((mom.me + ahead) % size))
+    source_gather = Gather(col, sbuf, sems_of(ag_sems, 1), near=True)
+    source_gather.start()
     to_behind.start()
     to_ahead.start()
-    source_gather = Gather(col, sbuf, src, sems_of(ag_sems, 1))
-    source_gather.start()
-    weight_gather = Gather(col, wbuf, w_in, sems_of(w_sems, 0))
+    weight_gather = Gather(col, wbuf, sems_of(w_sems, 0), near=True)
     weight_gather.start()
-    sbuf[col.me] = src[...]
-    wbuf[col.me] = w_in[...]
 
     def turn_panel(k):
-        v_copy(k).wait()
         rows = pl.ds(pl.multiple_of(k * panel, panel), panel)
         for n in range(groups):
             cols = slice(n * panel, (n + 1) * panel)
             v_turned[cols, rows] = v_mat[rows, cols].T
 
-    def forward_and_turn(k):
-        source_gather.forward(k)
-        turn_panel(k)
-
-    loop(groups - 1, forward_and_turn)
-    turn_panel(groups - 1)
+    early = min(3, groups - 1)
+    loop(groups, lambda k: v_copy(k).wait())
+    loop(early, turn_panel)
+    source_gather.forward_all()
     weight_gather.forward_all()
 
     to_behind.wait()
     to_ahead.wait()
     b_full[...] = -0.5 * (g_in[...] * s_ahead[...] + s_in[...] * g_behind[...])
-    source_gather.finish()
 
     def first_operand(k):
         two = sbuf[pl.ds(2 * k, 2)].astype(F32)
@@ -237,7 +238,8 @@
             part = two[:, :, n * LANES : (n + 1) * LANES].reshape(2 * ROWS, LANES)
             x_col[n, rows, :] = (part * b_full[n : n + 1, :]).astype(BF16)
 
-    loop(groups, first_operand)
+    source_gather.finish(first_operand)
+    source_gather.drain()
 
     here = pl.ds(pl.multiple_of(col.me * LANES, LANES), LANES)
     mine = sbuf[:, :, here].astype(F32).reshape(sources, LANES)
@@ -260,10 +262,12 @@
         cols = pl.ds(pl.multiple_of(d * panel, panel), panel)
         return jnp.dot(lhs, w[:, cols], preferred_element_type=F32)
 
-    def summed(a, x, w):
+    def summed(a, x, w, lag, meanwhile=None):
+        lag = min(lag, groups - 1)
+
         def pair_copy(k):
             return remote(
-                give.at[k], taken.at[a.which, k], rp_send.at[k], rp_recv.at[a.which, k], a.at(a.pair)
+                give.at[k], taken.at[a.which, k], rp_send.at[0, k], rp_recv.at[a.which, k], a.at(a.pair)
             )
 
         def mate_copy(k):
@@ -271,7 +275,7 @@
             return remote(
                 hand.at[k],
                 landed.at[a.which, t],
-                rg_send.at[k],
+                rg_send.at[0, k],
                 rg_recv.at[a.which, t],
                 a.at(a.mate(t)),
             )
@@ -285,14 +289,20 @@
             give[k] = jnp.where(first, high, low).astype(BF16)
             pair_copy(k).start()
 
-        loop(groups, multiply)
-
         def hand_on(k):
             pair_copy(k).wait_recv()
             hand[k] = (keep[k] + taken[a.which, k].astype(F32)).astype(BF16)
             mate_copy(k).start()
 
-        loop(groups - 1, hand_on)
+        def both_stages(k):
+            multiply(k + lag)
+            hand_on(k)
+
+        loop(lag, multiply)
+        loop(groups - lag, both_stages)
+        loop(lag - 1, lambda k: hand_on(k + groups - lag))
+        if meanwhile is not None:
+            meanwhile()
         pair_copy(groups - 1).wait_recv()
         total = keep[groups - 1] + taken[a.which, groups - 1].astype(F32)
 
@@ -308,11 +318,13 @@
 
         return total, sent
 
-    mom_gather = Gather(mom, x_mom, x_mom.at[mom.me], sems_of(ag_sems, 0))
-    col_gather = Gather(col, x_col, x_col.at[col.me], sems_of(ag_sems, 1))
-    dv_gather = Gather(col, dvbuf, dvbuf.at[col.me], sems_of(dv_sems, 0))
-
-    total, sent = summed(mom, x_col, v_mat)
+    mom_gather = Gather(mom, x_mom, sems_of(ag_sems, 0), near=False)
+    col_gather = Gather(col, x_col, sems_of(ag_sems, 1), near=True)
+    dv_gather = Gather(col, dvbuf, sems_of(dv_sems, 0), near=True)
+
+    total, sent = summed(
+        mom, x_col, v_mat, 3, lambda: loop(groups - early, lambda k: turn_panel(k + early))
+    )
 
     @pl.when(off_diagonal)
     def _():
@@ -338,15 +350,18 @@
     mom_gather.forward_all()
     mom_gather.finish()
 
-    total, sent = summed(col, x_mom, v_turned)
+    total, sent = summed(col, x_mom, v_turned, 6)
+    mom_gather.drain()
     col_state(vec_sent[0:1, :], total)
     col_gather.start()
     sent()
     col_gather.forward_all()
     col_gather.finish()
     weight_gather.finish()
-
-    total, sent = summed(mom, x_col, v_mat)
+    weight_gather.drain()
+
+    total, sent = summed(mom, x_col, v_mat, 3)
+    col_gather.drain()
     ladder_first = mom_state(vec_mom[0:1, :], total)
     mom_gather.start()
     weights = wbuf[...].reshape(sources, LANES)
@@ -370,7 +385,8 @@
 
     mom_gather.finish()
 
-    total, sent = summed(col, x_mom, v_turned)
+    total, sent = summed(col, x_mom, v_turned, 6)
+    mom_gather.drain()
 
     @pl.when(off_diagonal)
     def _():
@@ -388,13 +404,20 @@
     dv_gather.forward_all()
     col_gather.finish()
 
-    total, sent = summed(mom, x_col, v_mat)
+    total, sent = summed(mom, x_col, v_mat, 3)
+    col_gather.drain()
     mom_state(dv_sent[1:2, :], total)
     mom_gather.start()
     sent()
     mom_gather.forward_all()
     dv_gather.finish()
+    dv_gather.drain()
     mom_gather.finish()
+
+    half = block // 2
+
+    def lanes(h):
+        return pl.ds(pl.multiple_of(h * half, half), half)
 
     def last_product(d):
         both = product(x_mom, v_turned, d)
@@ -403,47 +426,61 @@
         fin_wide[:, :, cols] = wide
         fin[:, :, cols] = wide.astype(BF16)
 
-    loop(groups, last_product)
-
-    def fin_pair(k):
+    def fin_pair(k, h):
         there = col.mate(col.order(k)) + 1 - 2 * col.parity
         return remote(
-            fin.at[there], fin_taken.at[k], rp_send.at[k], rp_recv.at[2, k], col.at(col.pair)
+            fin.at[there, :, lanes(h)],
+            fin_taken.at[k, :, lanes(h)],
+            rp_send.at[h, k],
+            rp_recv.at[2 + h, k],
+            col.at(col.pair),
         )
 
-    def fin_mate(k):
+    def fin_mate(k, h):
         t = col.order(k)
         return remote(
-            fin_hand.at[k], fin_landed.at[t], rg_send.at[k], rg_recv.at[2, t], col.at(col.mate(t))
+            fin_hand.at[k, :, lanes(h)],
+            fin_landed.at[t, :, lanes(h)],
+            rg_send.at[h, k],
+            rg_recv.at[2 + h, t],
+            col.at(col.mate(t)),
         )
 
-    loop(groups, lambda k: fin_pair(k).start())
-
-    def fin_sum(k):
-        fin_pair(k).wait_recv()
-        return fin_wide[col.mate(col.order(k))] + fin_taken[k].astype(F32)
-
-    def fin_on(k):
-        fin_hand[k] = fin_sum(k).astype(BF16)
-        fin_mate(k).start()
-
-    loop(groups - 1, fin_on)
-    own[...] = fin_sum(groups - 1) + src[...].astype(F32)
+    def fin_sum(k, h):
+        fin_pair(k, h).wait_recv()
+        kept = fin_wide[col.mate(col.order(k)), :, lanes(h)]
+        return kept + fin_taken[k, :, lanes(h)].astype(F32)
+
+    def fin_on(k, h):
+        fin_hand[k, :, lanes(h)] = fin_sum(k, h).astype(BF16)
+        fin_mate(k, h).start()
+
+    def fin_half(h):
+        loop(groups // 2, lambda k: last_product(h * (groups // 2) + k))
+        loop(groups, lambda k: fin_pair(k, h).start())
+
+    loop(2, fin_half)
+    mom_gather.drain()
+    for h in range(2):
+        loop(groups - 1, lambda k, h=h: fin_on(k, h))
+        own[:, lanes(h)] = fin_sum(groups - 1, h) + sbuf[col.me, :, lanes(h)].astype(F32)
 
     for n in range(size):
         dre_out[n : n + 1, :] = dvbuf[n, 0:1, :]
 
-    def fin_add(k):
-        fin_mate(k).wait_recv()
-        own[...] += fin_landed[col.order(k)].astype(F32)
-
-    loop(groups - 1, fin_add)
+    def fin_add(k, h):
+        fin_mate(k, h).wait_recv()
+        own[:, lanes(h)] += fin_landed[col.order(k), :, lanes(h)].astype(F32)
+
+    for h in range(2):
+        loop(groups - 1, lambda k, h=h: fin_add(k, h))
     for n in range(size):
         cols = slice(n * LANES, (n + 1) * LANES)
         lad_out[:, cols] = dvbuf[n, 1:2, :] * own[:, cols]
 
-    loop(groups, lambda k: fin_pair(k).wait_send())
-    loop(groups - 1, lambda k: fin_mate(k).wait_send())
+    for h in range(2):
+        loop(groups, lambda k, h=h: fin_pair(k, h).wait_send())
+        loop(groups - 1, lambda k, h=h: fin_mate(k, h).wait_send())
 
 
 def ladder_call(size, ahead):
@@ -483,6 +520,10 @@
         pltpu.VMEM((ROWS, LANES), F32),
         pltpu.VMEM((ROWS, LANES), F32),
         pltpu.VMEM((ROWS, LANES), F32),
+        pltpu.VMEM((size, LANES), F32),
+        pltpu.VMEM((size, LANES), F32),
+        pltpu.SMEM((ROWS,), F32),
+        dma((4,)),
         dma((groups,)),
         dma((2,)),
         dma((2,)),
@@ -493,10 +534,10 @@
         dma((2, 4, groups)),
         dma((1, 4, groups)),
         dma((1, 4, groups)),
-        dma((groups,)),
-        dma((3, groups)),
-        dma((groups,)),
-        dma((3, groups)),
+        dma((2, groups)),
+        dma((4, groups)),
+        dma((2, groups)),
+        dma((4, groups)),
     ]
     return pl.pallas_call(
         functools.partial(kernel, size, ahead),
@@ -504,7 +545,7 @@
             jax.ShapeDtypeStruct((ROWS, block), F32),
             jax.ShapeDtypeStruct((size, LANES), F32),
         ),
-        in_specs=[pl.BlockSpec(memory_space=pl.ANY)] + [vmem] * 4,
+        in_specs=[pl.BlockSpec(memory_space=pltpu.HBM)] * 5,
         out_specs=(vmem, vmem),
         scratch_shapes=scratch,
         compiler_params=pltpu.CompilerParams(
@@ -517,13 +558,11 @@
 def body(ahead, vertex, sources, green_fn, green_shifted, leg_weights):
     size = lax.axis_size("mom")
     in_lanes = (size, LANES)
-    ladder, dressed = ladder_call(size, ahead)(
-        vertex,
-        sources,
-        green_fn.reshape(in_lanes),
-        green_shifted.reshape(in_lanes),
-        jnp.broadcast_to(leg_weights[:, None], (ROWS, LANES)),
-    )
+    in_hbm = [
+        pltpu.with_memory_space_constraint(x, pltpu.HBM)
+        for x in (vertex, sources, green_fn.reshape(in_lanes), green_shifted.reshape(in_lanes), leg_weights)
+    ]
+    ladder, dressed = ladder_call(size, ahead)(*in_hbm)
     return ladder, dressed.reshape(-1)
 
 

time: 142 us -> 137 us (0.965)
  local copies, waits for them, and re-layouts: 4.11 us -> 1.23 us
  Pallas kernels: 137 us -> 135 us
    pallas_call x1, Pallas kernels: 137 us -> 135 us  [body(): ladder, dressed = ladder_call(size, ahead)(*in_hbm)]
    unnamed x8 -> x2, local copies, waits for them, and re-layouts: 3.38 us -> 1.23 us
where the time goes in v2:
time: 137 us; the launch traced here: 136 us
  Pallas kernels  135 us (99%)
    pallas_call x1, Pallas kernels, body(): ladder, dressed = ladder_call(size, ahead)(*in_hbm)  135 us

profile of v2, /device:TPU:1, one launch (start us, length us, event | category | flops | bytes accessed | tf_op | source)
XLA Modules:
  0.0 136.5 jit_solution(15904068740994255372)
XLA Ops:
  0.6 134.6 %ladder.1 = (f32[8,2048]{1,0:T(8,128)S(1)}, f32[16,128]{1,0:T(8,128)S(1)}) custom-call(bf16[2048,2048]{1,0:T(8,128)(2,1)} %v_hbm.1, bf16[8,2048]{1,0:T(8,128)(2,1)} %src_hbm.1, f32[16,128]{1,0:T(8,128)} %bitcast.4, f32[16,128]{1,0:T(8,128)} %bitcast.5, f32[8]{0:T(128)} %w_hbm.1), custom_call_target="tpu_custom_call" | custom-call | tf_op jit(solution)/shard_map/ladder/pallas_call | solution.py:565
  135.3 0.6 copy.9
  135.9 0.6 copy.10

commit v3 on v2

--- a/solution.py
+++ b/solution.py
@@ -32,6 +32,10 @@
         return 2 * ((self.group + steps) % self.groups) + self.parity
 
     def order(self, k):
+        if self.which == 0 and self.groups == 8:
+            late, rest = k // 4, k % 4
+            sign = (1 - 2 * (rest % 2)) * (1 - 2 * late)
+            return (5 - late + sign * 2 * ((rest + 1) // 2) + 8) % 8
         sign = 2 * (k % 2) - 1
         return (self.groups // 2 + sign * ((k + 1) // 2) + self.groups) % self.groups
 

time: 137 us -> 133 us (0.971)
  Pallas kernels: 135 us -> 131 us
    pallas_call x1, Pallas kernels: 135 us -> 131 us  [body(): ladder, dressed = ladder_call(size, ahead)(*in_hbm)]
where the time goes in v3:
time: 133 us
  Pallas kernels  131 us (98%)
    pallas_call x1, Pallas kernels, body(): ladder, dressed = ladder_call(size, ahead)(*in_hbm)  131 us

profile of v3, /device:TPU:1, one launch (start us, length us, event | category | flops | bytes accessed | tf_op | source)
XLA Modules:
  0.0 132.9 jit_solution(450013179039818226)
XLA Ops:
  0.6 131.0 %ladder.1 = (f32[8,2048]{1,0:T(8,128)S(1)}, f32[16,128]{1,0:T(8,128)S(1)}) custom-call(bf16[2048,2048]{1,0:T(8,128)(2,1)} %v_hbm.1, bf16[8,2048]{1,0:T(8,128)(2,1)} %src_hbm.1, f32[16,128]{1,0:T(8,128)} %bitcast.4, f32[16,128]{1,0:T(8,128)} %bitcast.5, f32[8]{0:T(128)} %w_hbm.1), custom_call_target="tpu_custom_call" | custom-call | tf_op jit(solution)/shard_map/ladder/pallas_call | solution.py:569
  131.6 0.6 copy.9
  132.3 0.6 copy.10
